TPU v7x, 32 devices: a whole 2x2x4 slice. The times are simulated.
32 devices in a mesh: seq: 8 (over z, y), tp: 4 (over x, core).
Axes of the slice: x: 2, y: 2, z: 4, core: 2. Of those that a mesh axis runs over, the one named last changes fastest.
Arguments:
- tokens: bfloat16 [4096, 2048], P('seq'), may hold values from -16 to 16
- forget: float32 [4096, 32], P('seq', 'tp'), may hold values from -5 to 0, as said below
- attn_gain: float32 [2048], replicated, may hold values from 0.1 to 1.9
- projections: bfloat16 [3, 2048, 2048], P(None, None, 'tp'), may hold values from -0.125 to 0.125
- out_weight: bfloat16 [2048, 2048], P('tp'), may hold values from -0.125 to 0.125
- ffn_gain: float32 [2048], replicated, may hold values from 0.1 to 1.9
- expand_weight: bfloat16 [2, 2048, 4096], P(None, None, 'tp'), may hold values from -0.125 to 0.125
- down_weight: bfloat16 [4096, 2048], P('tp'), may hold values from -0.09375 to 0.09375
Outputs:
- output: bfloat16 [4096, 2048], P('seq')
Inputs may be any that keep to these rules, and one draw needn't show every extreme that they name: forget is never positive.
All inputs are finite; a program needn't handle non-finite values.
Results may differ from a plain program's by a relative error of at most 0.011.
Values may be sent and summed in bfloat16 or wider, within the bound.
A program may use at most 128 MiB of HBM per device.

v0:
```python
import math

import jax
import jax.numpy as jnp
from jax import lax
from jax.sharding import PartitionSpec as P

norm_epsilon = 1e-05
head_epsilon = 1e-06


def carried_in(value, axis, join, neutral):
    count, mine = (lax.axis_size(axis), lax.axis_index(axis))
    pieces = jax.tree.map(lambda part: lax.all_gather(part, axis), value)
    running = jax.tree.map(
        lambda part, zero: jnp.full_like(part, 0) + jnp.asarray(zero, part.dtype), value, neutral
    )

    def hop(position, running):
        longer = join(running, jax.tree.map(lambda part: part[position], pieces))
        return jax.tree.map(lambda new, old: jnp.where(position < mine, new, old), longer, running)

    return lax.fori_loop(0, count - 1, hop, running)


def rms_scale(values, gain_vector):
    widened = values.astype(jnp.float32)
    mean_square = jnp.mean(widened * widened, axis=-1, keepdims=True)
    return (widened * lax.rsqrt(mean_square + norm_epsilon) * gain_vector).astype(jnp.bfloat16)


def summarize(key_rows, value_rows, forget_rows):
    log_decay = jnp.cumsum(forget_rows, axis=0)
    block_total = log_decay[-1]
    shrink_factors = jnp.exp(block_total[None, :] - log_decay)
    scaled_keys = (key_rows.astype(jnp.float32) * shrink_factors[:, :, None]).astype(jnp.bfloat16)
    block_state = jnp.einsum(
        "shd,she->hde", scaled_keys, value_rows, preferred_element_type=jnp.float32
    )
    return (log_decay, block_total, block_state)


def local_attention(query_rows, key_rows, value_rows, log_decay):
    head_size = query_rows.shape[2]
    score_scale = 1.0 / math.sqrt(head_size)
    scores = (
        jnp.einsum("thd,shd->hts", query_rows, key_rows, preferred_element_type=jnp.float32)
        * score_scale
    )
    log_gaps = log_decay.T[:, :, None] - log_decay.T[:, None, :]
    row_order = jnp.arange(query_rows.shape[0])
    causal = (row_order[:, None] >= row_order[None, :])[None]
    local_weights = jnp.where(
        causal, scores * jnp.exp(jnp.where(causal, log_gaps, 0.0)), 0.0
    ).astype(jnp.bfloat16)
    return jnp.einsum("hts,she->the", local_weights, value_rows, preferred_element_type=jnp.float32)


def finish_heads(query_rows, local_part, log_decay, incoming):
    head_size = query_rows.shape[2]
    score_scale = 1.0 / math.sqrt(head_size)
    carried = jnp.einsum(
        "thd,hde->the", query_rows.astype(jnp.float32), incoming, precision=lax.Precision.HIGHEST
    )
    attended = local_part + carried * (jnp.exp(log_decay) * score_scale)[:, :, None]
    mean_square = jnp.mean(attended * attended, axis=-1, keepdims=True)
    head_out = (attended * lax.rsqrt(mean_square + head_epsilon)).astype(jnp.bfloat16)
    return head_out.reshape(query_rows.shape[0], -1)


def feed_forward(rows_in, expand_weight):
    gate_proj = jnp.dot(rows_in, expand_weight[0], preferred_element_type=jnp.float32)
    up_proj = jnp.dot(rows_in, expand_weight[1], preferred_element_type=jnp.float32)
    return (jax.nn.silu(gate_proj) * up_proj).astype(jnp.bfloat16)


def local(tokens, forget, attn_gain, projections, out_weight, ffn_gain, expand_weight, down_weight):
    row_count = tokens.shape[0]
    head_count = forget.shape[1]
    head_size = projections.shape[2] // head_count
    normed = rms_scale(tokens, attn_gain)
    shaped = []
    for which in range(3):
        projected = jnp.dot(normed, projections[which], preferred_element_type=jnp.float32).astype(
            jnp.bfloat16
        )
        shaped.append(projected.reshape(row_count, head_count, head_size))
    query_rows, key_rows, value_rows = shaped
    log_decay, block_total, block_state = summarize(key_rows, value_rows, forget)

    def combine(earlier, following):
        return (earlier[0] * following[0], following[0][:, None, None] * earlier[1] + following[1])

    identity = (jnp.ones_like(block_total), jnp.zeros_like(block_state))
    _, incoming = carried_in((jnp.exp(block_total), block_state), "seq", combine, identity)
    local_part = local_attention(query_rows, key_rows, value_rows, log_decay)
    head_out = finish_heads(query_rows, local_part, log_decay, incoming)
    row_share = row_count // lax.axis_size("tp")
    tp_index = lax.axis_index("tp")
    own_tokens = lax.dynamic_slice_in_dim(tokens, tp_index * row_share, row_share, 0)
    picked = head_out
    attn_summed = lax.psum_scatter(
        jnp.dot(picked, out_weight, preferred_element_type=jnp.float32),
        "tp",
        scatter_dimension=0,
        tiled=True,
    )
    residual = (own_tokens.astype(jnp.float32) + attn_summed).astype(jnp.bfloat16)
    normed_ffn = rms_scale(residual, ffn_gain)
    hidden = feed_forward(lax.all_gather(normed_ffn, "tp", axis=0, tiled=True), expand_weight)
    picked = hidden
    ffn_summed = lax.psum_scatter(
        jnp.dot(picked, down_weight, preferred_element_type=jnp.float32).astype(jnp.bfloat16),
        "tp",
        scatter_dimension=0,
        tiled=True,
    ).astype(jnp.float32)
    own_output = (residual.astype(jnp.float32) + ffn_summed).astype(jnp.bfloat16)
    return lax.all_gather(own_output, "tp", axis=0, tiled=True)


def solution(mesh):
    placed = (
        P("seq", None),
        P("seq", "tp"),
        P(),
        P(None, None, "tp"),
        P("tp", None),
        P(),
        P(None, None, "tp"),
        P("tp", None),
    )
    return jax.shard_map(
        local, mesh=mesh, in_specs=placed, out_specs=P("seq", None), check_vma=False
    )
```

profile of v0, /device:TPU:17, one launch (start us, length us, event | category | flops | bytes accessed | tf_op | source)
XLA Modules:
  0.0 233.7 jit_solution(2786294146817347962)
XLA Ops:
  6.5 2.2 fusion.1
  8.8 3.8 %fusion.34 = bf16[512,512]{0,1:T(8,128)(2,1)S(1)} fusion(bf16[3,2048,512]{2,1,0:T(8,128)(2,1)} %param.13, bf16[512,2048]{1,0:T(8,128)(2,1)} %param.10, f32[2048]{0:T(1024)} %param.12, f32[512]{0:T(512)S(1)} %add_rsqrt_fusion.1), kind=kOutput, calls=%fused_computation.38 | convolution fusion | flops 1078198272 | bytes 4728832 | tf_op jit(solution)/shard_map/dot_general | solution.py:84
  12.6 3.2 %fusion.28 = bf16[512,512]{0,1:T(8,128)(2,1)S(1)} fusion(bf16[3,2048,512]{2,1,0:T(8,128)(2,1)} %param.13, bf16[512,2048]{1,0:T(8,128)(2,1)S(1)} %copy-done.1, f32[2048]{0:T(1024)S(1)} %copy-done.6, f32[512]{0:T(512)S(1)} %add_rsqrt_fusion.1), kind=kOutput, calls=%fused_computation.36 | convolution fusion | flops 1078198272 | bytes 4728832 | tf_op jit(solution)/shard_map/dot_general | solution.py:84
  15.9 1.1 reduce-window.6
  18.7 11.8 %all-gather.1 = f32[8,1,8]{2,1,0:T(1,128)S(1)} all-gather(f32[1,1,8]{2,1,0:T(1,128)S(1)} %bitcast.80), channel_id=1, replica_groups=mesh['seq'=8,'tp'=4] {'seq'}, dimensions={0}, use_global_device_ids=true | all-gather | bytes 288 | tf_op jit(solution)/shard_map/all_gather | solution.py:14
  31.3 4.4 %fusion.31 = bf16[512,512]{0,1:T(8,128)(2,1)} fusion(bf16[3,2048,512]{2,1,0:T(8,128)(2,1)} %param.13, bf16[512,2048]{1,0:T(8,128)(2,1)} %param.10, f32[2048]{0:T(1024)S(1)} %copy-done.6, f32[512]{0:T(512)S(1)} %add_rsqrt_fusion.1), kind=kOutput, calls=%fused_computation.37 | convolution fusion | flops 1078198272 | bytes 4728832 | tf_op jit(solution)/shard_map/dot_general | solution.py:84
  35.7 5.4 %fusion.25 = f32[512,8,64]{0,2,1:T(8,128)S(1)} fusion(bf16[512,8,64]{0,2,1:T(8,128)(2,1)} %bitcast.77, f32[8,512]{1,0:T(8,128)S(1)} %add_bitcast_fusion.1, pred[512,512]{1,0:T(8,128)(4,1)} %iota_compare_fusion, bf16[512,8,64]{0,2,1:T(8,128)(2,1)} %bitcast.72, bf16[512,8,64]{0,2,1:T(8,128)(2,1)} %bitcast.75), kind=kOutput, calls=%fused_computation.32 | convolution fusion | flops 549453824 | bytes 2899968 | tf_op jit(solution)/shard_map/hts,she->the/dot_general | solution.py:56
  41.1 26.7 %all-gather.10.cloned.1.call-done = f32[64,64,64]{2,1,0:T(8,128)} async-done(((f32[8,64,64]{2,1,0:T(8,128)}), f32[64,64,64]{2,1,0:T(8,128)}) %all-gather.10.cloned.1.call-update) | async-done | bytes 1048592 | tf_op jit(solution)/shard_map/all_gather | solution.py:14
  67.8 7.6 %while.14 = (s32[]{:T(128)}, f32[8,64,64]{2,1,0:T(8,128)S(1)}, s32[]{:T(128)}, f32[8,8]{1,0:T(8,128)S(1)}, f32[8,8,64,64]{3,2,1,0:T(8,128)}, /*index=5*/s32[]{:T(128)}, s32[]{:T(128)}) while((s32[]{:T(128)}, f32[8,64,64]{2,1,0:T(8,128)S(1)}, s32[]{:T(128)}, f32[8,8]{1,0:T(8,128)S(1)}, f32[8,8,64,64]{3,2,1,0:T(8,128)}, ...), condition=%wide.region_4.5_spmd.clone, body=%wide.region_3.4_spmd.clone.sunk | while | flops 131076 | bytes 393425 | solution.py:23
  68.9 1.1 fusion.65
  71.1 1.1 fusion.65
  72.2 1.1 fusion.65
  73.3 1.1 fusion.65
  75.5 1.8 multiply_reduce_fusion
  77.4 3.2 %fusion.52 = f32[512,2048]{1,0:T(8,128)} fusion(bf16[512,512]{0,1:T(8,128)(2,1)S(1)} %bitcast.70, bf16[512,2048]{1,0:T(8,128)(2,1)S(1)} %copy-done), kind=kOutput, calls=%fused_computation.64 | convolution fusion | flops 1073741824 | bytes 6815744 | tf_op jit(solution)/shard_map/dot_general | solution.py:103
  80.7 44.3 %reduce-scatter.3.cloned.1.call-done = f32[128,2048]{1,0:T(8,128)} async-done(((f32[512,2048]{1,0:T(8,128)}), f32[128,2048]{1,0:T(8,128)}) %reduce-scatter.3.cloned.1.call-update) | async-done | bytes 1048592 | tf_op jit(solution)/shard_map/reduce_scatter | solution.py:102
  125.0 1.6 fusion.39
  127.9 23.1 %all-gather.6.cloned.1.call-done = bf16[512,2048]{1,0:T(8,128)(2,1)} async-done(((bf16[128,2048]{1,0:T(8,128)(2,1)}), bf16[512,2048]{1,0:T(8,128)(2,1)}) %all-gather.6.cloned.1.call-update) | async-done | bytes 2097168 | tf_op jit(solution)/shard_map/all_gather | solution.py:110
  150.9 6.5 %fusion.6 = f32[512,1024]{1,0:T(8,128)} fusion(bf16[512,2048]{1,0:T(8,128)(2,1)} %all-gather.6.cloned.1.call-done, bf16[2,2048,1024]{2,1,0:T(8,128)(2,1)} %param.16), kind=kOutput, calls=%fused_computation.11 | convolution fusion | flops 2147483648 | bytes 8388608 | tf_op jit(solution)/shard_map/dot_general | solution.py:72
  157.4 10.6 %convolution_convert_fusion = bf16[512,2048]{1,0:T(8,128)(2,1)} fusion(bf16[1024,2048]{1,0:T(8,128)(2,1)} %param.17, f32[512,1024]{1,0:T(8,128)} %fusion.6, bf16[512,2048]{1,0:T(8,128)(2,1)} %all-gather.6.cloned.1.call-done, bf16[2,2048,1024]{2,1,0:T(8,128)(2,1)} %param.16), kind=kOutput, calls=%fused_computation.18 | convolution fusion | flops 4299161600 | bytes 14680064 | tf_op jit(solution)/shard_map/dot_general | solution.py:113
  168.1 30.7 %reduce-scatter.5.cloned.1.call-done = bf16[128,2048]{1,0:T(8,128)(2,1)} async-done(((bf16[512,2048]{1,0:T(8,128)(2,1)}), bf16[128,2048]{1,0:T(8,128)(2,1)}) %reduce-scatter.5.cloned.1.call-update) | async-done | bytes 524304 | tf_op jit(solution)/shard_map/reduce_scatter | solution.py:112
  198.8 2.0 fusion.42
  200.8 23.3 %all-gather.8.cloned.1.call-done = bf16[512,2048]{1,0:T(8,128)(2,1)} async-done(((bf16[128,2048]{1,0:T(8,128)(2,1)}), bf16[512,2048]{1,0:T(8,128)(2,1)}) %all-gather.8.cloned.1.call-update) | async-done | bytes 2097168 | tf_op jit(solution)/shard_map/all_gather | solution.py:119
  224.1 3.2 %copy.25 = bf16[512,2048]{1,0:T(8,128)(2,1)} copy(bf16[512,2048]{1,0:T(8,128)(2,1)} %all-gather.8.cloned.1.call-done) | data formatting | bytes 4194304
  (49 shorter events, 7.2 us)
Async XLA Ops:
  6.5 70.9 %copy-start = (bf16[512,2048]{1,0:T(8,128)(2,1)S(1)}, bf16[512,2048]{1,0:T(8,128)(2,1)}, u32[]{:S(2)}) copy-start(bf16[512,2048]{1,0:T(8,128)(2,1)} %param.14) | copy-start | bytes 6291460
  6.5 61.3 %all-gather.10.cloned.1.call-start = ((), (), s32[]{:S(2)}) async-start(), calls=%async_computation.6 | async-start | bytes 2359296 | tf_op jit(solution)/shard_map/all_gather | solution.py:14
  8.8 3.8 %copy-start.1 = (bf16[512,2048]{1,0:T(8,128)(2,1)S(1)}, bf16[512,2048]{1,0:T(8,128)(2,1)}, u32[]{:S(2)}) copy-start(bf16[512,2048]{1,0:T(8,128)(2,1)} %param.10) | copy-start | bytes 6291460
  8.8 3.8 %copy-start.6 = (f32[2048]{0:T(1024)S(1)}, f32[2048]{0:T(1024)}, u32[]{:S(2)}) copy-start(f32[2048]{0:T(1024)} %param.12) | copy-start | bytes 24580
  12.6 5.0 %copy-start.2 = (bf16[512,512]{0,1:T(8,128)(2,1)}, bf16[512,512]{0,1:T(8,128)(2,1)S(1)}, u32[]{:S(2)}) copy-start(bf16[512,512]{0,1:T(8,128)(2,1)S(1)} %fusion.34) | copy-start | bytes 1572868
  12.6 3.3 %copy-start.4 = (f32[512,8]{0,1:T(8,128)S(1)}, f32[512,8]{0,1:T(8,128)}, u32[]{:S(2)}) copy-start(f32[512,8]{0,1:T(8,128)} %param.11) | copy-start | bytes 49156
  15.8 19.9 %copy-start.3 = (bf16[512,512]{0,1:T(8,128)(2,1)}, bf16[512,512]{0,1:T(8,128)(2,1)S(1)}, u32[]{:S(2)}) copy-start(bf16[512,512]{0,1:T(8,128)(2,1)S(1)} %fusion.28) | copy-start | bytes 1572868
  18.6 106.4 %reduce-scatter.3.cloned.1.call-start = ((), (), s32[]{:S(2)}) async-start(), calls=%async_computation.2 | async-start | bytes 5242880 | tf_op jit(solution)/shard_map/reduce_scatter | solution.py:102
  80.6 46.0 %copy-start.5 = (f32[2048]{0:T(1024)S(1)}, f32[2048]{0:T(1024)}, u32[]{:S(2)}) copy-start(f32[2048]{0:T(1024)} %param.15) | copy-start | bytes 24580
  80.7 70.3 %all-gather.6.cloned.1.call-start = ((), (), s32[]{:S(2)}) async-start(), calls=%async_computation.3 | async-start | bytes 2621440 | tf_op jit(solution)/shard_map/all_gather | solution.py:110
  127.7 71.1 %reduce-scatter.5.cloned.1.call-start = ((), (), s32[]{:S(2)}) async-start(), calls=%async_computation.4 | async-start | bytes 2621440 | tf_op jit(solution)/shard_map/reduce_scatter | solution.py:112
  168.0 56.0 %all-gather.8.cloned.1.call-start = ((), (), s32[]{:S(2)}) async-start(), calls=%async_computation.5 | async-start | bytes 2621440 | tf_op jit(solution)/shard_map/all_gather | solution.py:119
Sparse Core Ops, SparseCore 0:
  18.7 49.0 all-gather.9
  80.8 44.1 reduce-scatter.2
  127.8 23.1 all-gather.5
  168.1 30.6 reduce-scatter.4
  200.9 23.1 all-gather.7
where the time goes:
time: 236 us; the launch traced here: 234 us
  waiting for transfers between devices  148 us (63%)
  matrix products  39.9 us (17%)
  other arithmetic  16.5 us (7%)
  between operations  13.3 us (6%)
  blocking collectives  11.8 us (5%)
  local copies, waits for them, and re-layouts  3.6 us (2%)
    reduce_scatter x1, waiting for transfers between devices, local(): lax.psum_scatter(jnp.dot(picked, out_weight, preferred_element_type=jnp.f...  44.3 us
    reduce_scatter x1, waiting for transfers between devices, local(): lax.psum_scatter(jnp.dot(picked, down_weight, preferred_element_type=jnp....  30.7 us
    all_gather x1, waiting for transfers between devices, carried_in(): pieces = jax.tree.map(lambda part: lax.all_gather(part, axis), value)  26.7 us
    all_gather x1, waiting for transfers between devices, local(): return lax.all_gather(own_output, 'tp', axis=0, tiled=True)  23.3 us
    all_gather x1, waiting for transfers between devices, local(): lax.all_gather(normed_ffn, 'tp', axis=0, tiled=True)  23.1 us
    all_gather x1, blocking collectives, carried_in(): pieces = jax.tree.map(lambda part: lax.all_gather(part, axis), value)  11.8 us
    dot_general x3, matrix products, local(): jnp.dot(normed, projections[which], preferred_element_type=jnp.float32)  11.4 us
    dot_general x1, matrix products, local(): jnp.dot(picked, down_weight, preferred_element_type=jnp.float32)  10.6 us
  transfers between devices with their start and end apart: 5, of which 5 were waited for; matrix products, arithmetic and copies ran while one was open for 5% of the time, Pallas kernels for 0%

commit v1 on v0

v1 whole, which is shorter than its diff:
```python
import functools

import jax
import jax.numpy as jnp
from jax import lax
from jax.experimental import pallas as pl
from jax.experimental.pallas import tpu as pltpu
from jax.sharding import PartitionSpec as P

norm_epsilon = 1e-05
head_epsilon = 1e-06
MESH = pl.DeviceIdType.MESH
CHUNKS = 4
F32 = jnp.float32
BF16 = jnp.bfloat16


def dot(a, b):
    return jnp.dot(a, b, preferred_element_type=F32)


def contract(a, b, dim_a, dim_b):
    return lax.dot_general(
        a, b, (((dim_a,), (dim_b,)), ((), ())), preferred_element_type=F32
    )


def normalize(widened, gain):
    mean_square = jnp.mean(widened * widened, axis=-1, keepdims=True)
    return (widened * lax.rsqrt(mean_square + norm_epsilon) * gain).astype(BF16)


def kernel(
    blocks, steps,
    tok_hbm, fg, fgt, again, proj_hbm, ow_hbm, fgain, ew_hbm, dw_hbm,
    out_hbm,
    tok, wq, wk, wv, wo, wg, wu, wd,
    normed, q, k, v, att, ho, bd, es, el, ts, tl, tsb, tsl, trb, trl,
    part, own, dsend1, drecv1, xsend1, xrecv1, nf, res, hid,
    dsend2, drecv2, xsend2, xrecv2, outb,
    ld, ldt,
    wsem, sts, strv, d1s, d1r, x1s, x1r, ns, nr, d2s, d2r, x2s, x2r, osd, orv, olc,
):
    rows, width = tok.shape
    heads = fg.shape[1]
    pairs = heads // 2
    chunk = rows // CHUNKS
    half = chunk // 2
    me = lax.axis_index("seq")
    tp = lax.axis_index("tp")
    core = lax.rem(tp, 2)
    partner = tp + 1 - 2 * core
    across = lax.rem(tp + 2, 4)

    loads = []
    for at, (src, dst) in enumerate((
        (tok_hbm, tok), (proj_hbm.at[1], wk), (proj_hbm.at[2], wv), (proj_hbm.at[0], wq),
        (ow_hbm, wo), (ew_hbm.at[0], wg), (ew_hbm.at[1], wu), (dw_hbm, wd),
    )):
        copy = pltpu.make_async_copy(src, dst, wsem.at[at])
        copy.start()
        loads.append(copy)

    barrier = pltpu.get_barrier_semaphore()
    for other in (partner, across):
        pl.semaphore_signal(barrier, inc=1, device_id={"tp": other}, device_id_type=MESH)
    for step in range(steps):
        for far in (2 ** step, blocks - 2 ** step):
            pl.semaphore_signal(
                barrier, inc=1, device_id={"seq": lax.rem(me + far, blocks)}, device_id_type=MESH)

    tri = (
        lax.broadcasted_iota(jnp.int32, (rows, rows), 0)
        >= lax.broadcasted_iota(jnp.int32, (rows, rows), 1)
    ).astype(F32)
    ld[...] = lax.dot_general(
        tri, fg[...], (((1,), (0,)), ((), ())),
        precision=lax.Precision.HIGHEST, preferred_element_type=F32,
    )
    ldt[...] = lax.dot_general(
        fgt[...], tri, (((1,), (1,)), ((), ())),
        precision=lax.Precision.HIGHEST, preferred_element_type=F32,
    )

    loads[0].wait()

    def norm_chunk(r, carry):
        at = pl.ds(pl.multiple_of(r * chunk, chunk), chunk)
        normed[at, :] = normalize(tok[at, :].astype(F32), again[...])
        return carry

    lax.fori_loop(0, CHUNKS, norm_chunk, 0)

    def project(weight, dst):
        tile = min(256, dst.shape[1])

        def body(j, carry):
            at = pl.ds(pl.multiple_of(j * tile, tile), tile)
            dst[:, at] = dot(normed[...], weight[:, at]).astype(BF16)
            return carry

        lax.fori_loop(0, dst.shape[1] // tile, body, 0)

    loads[1].wait()
    project(wk, k)
    loads[2].wait()
    project(wv, v)

    low = lax.broadcasted_iota(jnp.int32, (1, 128), 1) < 64
    low_f = low.astype(F32)
    masks_f = (low_f, 1.0 - low_f)
    masks = (masks_f[0].astype(BF16), masks_f[1].astype(BF16))

    def spread(columns, p):
        return jnp.where(low, columns[:, 2 * p : 2 * p + 1], columns[:, 2 * p + 1 : 2 * p + 2])

    log_decay = ld[...]
    last = log_decay[rows - 1 : rows, :]
    shrink = jnp.exp(last - log_decay)
    tl[...] = jnp.zeros_like(tl)
    el[...] = jnp.zeros_like(el)
    es[...] = jnp.zeros_like(es)
    for p in range(pairs):
        lanes = slice(128 * p, 128 * p + 128)
        scaled = (k[:, lanes].astype(F32) * spread(shrink, p)).astype(BF16)
        state = contract(scaled, v[:, lanes], 0, 0)
        ts[64 * p : 64 * p + 64, :] = state[:64] * masks_f[0] + state[64:] * masks_f[1]
        tl[p : p + 1, :] = spread(last, p)

    pl.semaphore_wait(barrier, 2 + 2 * steps)

    def state_copies(step):
        far = 2 ** step
        return (
            pltpu.make_async_remote_copy(
                tsb.at[step], trb.at[step], sts.at[step, 0], strv.at[step, 0],
                device_id={"seq": me + far}, device_id_type=MESH),
            pltpu.make_async_remote_copy(
                tsl.at[step], trl.at[step], sts.at[step, 1], strv.at[step, 1],
                device_id={"seq": me + far}, device_id_type=MESH),
        )

    def send_state(step):
        @pl.when(me + 2 ** step < blocks)
        def _():
            tsb[step] = ts[...].astype(BF16)
            tsl[step] = tl[...]
            for copy in state_copies(step):
                copy.start()

    def take_state(step):
        @pl.when(me >= 2 ** step)
        def _():
            for copy in state_copies(step):
                copy.wait_recv()
            e_decay = jnp.exp(el[...])
            t_decay = jnp.exp(tl[...])
            for p in range(pairs):
                at = slice(64 * p, 64 * p + 64)
                came = trb[step, at, :].astype(F32)
                es[at, :] = es[at, :] + e_decay[p : p + 1, :] * came
                ts[at, :] = ts[at, :] + t_decay[p : p + 1, :] * came
            el[...] = el[...] + trl[step]
            tl[...] = tl[...] + trl[step]

        if step + 1 < steps:
            send_state(step + 1)

    if steps:
        send_state(0)
    loads[3].wait()
    project(wq, q)

    span = rows // 2
    taken = 0
    for p in range(pairs):
        lanes = slice(128 * p, 128 * p + 128)
        for piece in range(2):
            at = slice(piece * span, piece * span + span)
            reach = (piece + 1) * span
            causal = (
                lax.broadcasted_iota(jnp.int32, (span, reach), 0) + piece * span
                >= lax.broadcasted_iota(jnp.int32, (span, reach), 1)
            )
            sums = []
            for j in range(2):
                h = 2 * p + j
                scores = contract(q[at, lanes] * masks[j], k[:reach, lanes], 1, 1)
                gaps = jnp.where(causal, ld[at, h : h + 1] - ldt[h : h + 1, :reach], -1e30)
                weights = (scores * 0.125 * jnp.exp(gaps)).astype(BF16)
                sums.append(dot(weights, v[:reach, lanes]))
            att[at, lanes] = jnp.where(low, sums[0], sums[1])
        if taken < steps:
            take_state(taken)
            taken += 1
    while taken < steps:
        take_state(taken)
        taken += 1

    for p in range(pairs):
        came = es[64 * p : 64 * p + 64, :]
        bd[p] = jnp.concatenate([came * masks_f[0], came * masks_f[1]], axis=0).astype(BF16)
    same_head = (
        (lax.broadcasted_iota(jnp.int32, (128, 128), 0) < 64)
        == (lax.broadcasted_iota(jnp.int32, (128, 128), 1) < 64)
    ).astype(F32).astype(BF16)

    def whole_rows(r):
        return pl.ds(pl.multiple_of(r * chunk, chunk), chunk)

    def own_rows(r):
        return pl.ds(pl.multiple_of(r * chunk + core * half, half), half)

    mine = pl.ds(pl.multiple_of(core * half, half), half)
    theirs = pl.ds(pl.multiple_of(half - core * half, half), half)

    def to(src, dst, ssem, rsem, other):
        return pltpu.make_async_remote_copy(
            src, dst, ssem, rsem, device_id={"tp": other}, device_id_type=MESH)

    def d1(r):
        return to(dsend1.at[r], drecv1.at[r], d1s.at[r], d1r.at[r], partner)

    def x1(r):
        return to(xsend1.at[r], xrecv1.at[r], x1s.at[r], x1r.at[r], across)

    def nfc(r):
        return to(nf.at[own_rows(r)], nf.at[own_rows(r)], ns.at[r], nr.at[r], partner)

    def d2(r):
        return to(dsend2.at[r], drecv2.at[r], d2s.at[r], d2r.at[r], partner)

    def x2(r):
        return to(xsend2.at[r], xrecv2.at[r], x2s.at[r], x2r.at[r], across)

    def oc(r):
        return to(outb.at[r], out_hbm.at[own_rows(r)], osd.at[r], orv.at[r], partner)

    def ol(r):
        return pltpu.make_async_copy(outb.at[r], out_hbm.at[own_rows(r)], olc.at[r])

    loads[4].wait()
    wide = min(512, width)

    def attend(r, carry):
        at = whole_rows(r)
        reach_decay = jnp.exp(ld[at, :]) * 0.125
        for p in range(pairs):
            lanes = slice(128 * p, 128 * p + 128)
            attended = att[at, lanes] + dot(q[at, lanes], bd[p]) * spread(reach_decay, p)
            mean_square = dot((attended * attended).astype(BF16), same_head) * (1.0 / 64)
            ho[at, lanes] = (attended * lax.rsqrt(mean_square + head_epsilon)).astype(BF16)
        for c in range(width // wide):
            cols = slice(c * wide, c * wide + wide)
            part[:, cols] = dot(ho[at, :], wo[:, cols])
        own[r] = part[mine, :]
        dsend1[r] = part[theirs, :].astype(BF16)
        d1(r).start()
        return carry

    def cross1(r):
        d1(r).wait_recv()
        xsend1[r] = (own[r] + drecv1[r].astype(F32)).astype(BF16)
        x1(r).start()

    def attend_cross(r, carry):
        attend(r, 0)

        @pl.when(r > 0)
        def _():
            cross1(r - 1)

        return carry

    lax.fori_loop(0, CHUNKS, attend_cross, 0)
    cross1(CHUNKS - 1)
    for at in (5, 6, 7):
        loads[at].wait()

    hidden_width = wg.shape[1]
    tile = min(256, hidden_width)

    def forward(r, carry):
        x1(r).wait_recv()
        added = xsend1[r].astype(F32) + xrecv1[r].astype(F32)
        kept = (tok[own_rows(r), :].astype(F32) + added).astype(BF16)
        res[r] = kept
        nf[own_rows(r), :] = normalize(kept.astype(F32), fgain[...])
        nfc(r).start()
        nfc(r).wait_recv()
        at = whole_rows(r)
        for c in range(hidden_width // tile):
            cols = slice(c * tile, c * tile + tile)
            gate = dot(nf[at, :], wg[:, cols])
            up = dot(nf[at, :], wu[:, cols])
            hid[:, cols] = (gate / (1.0 + jnp.exp(-gate)) * up).astype(BF16)
        for c in range(width // wide):
            cols = slice(c * wide, c * wide + wide)
            part[:, cols] = dot(hid[...], wd[:, cols])
        own[r] = part[mine, :]
        dsend2[r] = part[theirs, :].astype(BF16)
        d2(r).start()
        d2(r).wait_recv()
        xsend2[r] = (own[r] + drecv2[r].astype(F32)).astype(BF16)
        x2(r).start()
        return carry

    lax.fori_loop(0, CHUNKS, forward, 0)

    def finish(r, carry):
        x2(r).wait_recv()
        added = xsend2[r].astype(F32) + xrecv2[r].astype(F32)
        outb[r] = (res[r].astype(F32) + added).astype(BF16)
        oc(r).start()
        ol(r).start()
        return carry

    lax.fori_loop(0, CHUNKS, finish, 0)

    def drain(r, carry):
        for copy in (d1(r), x1(r), nfc(r), d2(r), x2(r)):
            copy.wait_send()
        oc(r).wait()
        ol(r).wait()
        return carry

    lax.fori_loop(0, CHUNKS, drain, 0)
    for step in range(steps):
        @pl.when(me + 2 ** step < blocks)
        def _():
            for copy in state_copies(step):
                copy.wait_send()


def local(blocks, tokens, forget, attn_gain, projections, out_weight, ffn_gain, expand_weight, down_weight):
    rows, width = tokens.shape
    heads = forget.shape[1]
    inner = projections.shape[2]
    hidden = down_weight.shape[0]
    pairs = heads // 2
    steps = max(blocks - 1, 0).bit_length()
    chunk = rows // CHUNKS
    half = chunk // 2
    V = pltpu.VMEM
    S = pltpu.SemaphoreType.DMA
    slots = max(steps, 1)
    piece = V((CHUNKS, half, width), BF16)
    scratch = [
        V((rows, width), BF16),
        V((width, inner), BF16), V((width, inner), BF16), V((width, inner), BF16),
        V((inner, width), BF16),
        V((width, hidden), BF16), V((width, hidden), BF16), V((hidden, width), BF16),
        V((rows, width), BF16),
        V((rows, inner), BF16), V((rows, inner), BF16), V((rows, inner), BF16),
        V((rows, inner), F32), V((rows, inner), BF16),
        V((pairs, 128, 128), BF16),
        V((64 * pairs, 128), F32), V((8, 128), F32), V((64 * pairs, 128), F32), V((8, 128), F32),
        V((slots, 64 * pairs, 128), BF16), V((slots, 8, 128), F32),
        V((slots, 64 * pairs, 128), BF16), V((slots, 8, 128), F32),
        V((chunk, width), F32), V((CHUNKS, half, width), F32),
        piece, piece, piece, piece,
        V((rows, width), BF16), piece, V((chunk, hidden), BF16),
        piece, piece, piece, piece, piece,
        V((rows, heads), F32), V((heads, rows), F32),
        S((8,)), S((slots, 2)), S((slots, 2)),
    ] + [S((CHUNKS,)) for _ in range(13)]
    hbm = pl.BlockSpec(memory_space=pl.ANY)
    vmem = pl.BlockSpec(memory_space=pltpu.VMEM)
    return pl.pallas_call(
        functools.partial(kernel, blocks, steps),
        out_shape=jax.ShapeDtypeStruct((rows, width), BF16),
        in_specs=[hbm, vmem, vmem, vmem, hbm, hbm, vmem, hbm, hbm],
        out_specs=hbm,
        scratch_shapes=scratch,
        compiler_params=pltpu.CompilerParams(
            collective_id=0, has_side_effects=True, vmem_limit_bytes=64_000_000
        ),
    )(
        tokens, forget, forget.T, attn_gain[None, :], projections, out_weight,
        ffn_gain[None, :], expand_weight, down_weight,
    )


def solution(mesh):
    placed = (
        P("seq", None),
        P("seq", "tp"),
        P(),
        P(None, None, "tp"),
        P("tp", None),
        P(),
        P(None, None, "tp"),
        P("tp", None),
    )
    return jax.shard_map(
        functools.partial(local, mesh.shape["seq"]),
        mesh=mesh, in_specs=placed, out_specs=P("seq", None), check_vma=False,
    )
```

time: 236 us -> 74.1 us (0.31)
  waiting for transfers between devices: 148 us -> 0 us
  Pallas kernels: 0 us -> 69.2 us
  matrix products: 39.9 us -> 0 us
  other arithmetic: 16.5 us -> 0 us
  between operations: 13.3 us -> 0.01 us
  blocking collectives: 11.8 us -> 0 us
    reduce_scatter x2 -> x0, waiting for transfers between devices: 75 us -> none  [the longest x1 44.3 us: local(): lax.psum_scatter(jnp.dot(picked, out_weight, preferred_element_type=jnp.f...]
    all_gather x3 -> x0, waiting for transfers between devices: 73 us -> none  [the longest x1 26.7 us: carried_in(): pieces = jax.tree.map(lambda part: lax.all_gather(part, axis), value)]
    pallas_call x0 -> x1, Pallas kernels: none -> 69.2 us  [local(): pl.pallas_call(functools.partial(kernel, blocks, steps), out_shape=jax.Sh...]
    dot_general x9 -> x0, matrix products: 39.9 us -> none  [the longest x3 11.4 us: local(): jnp.dot(normed, projections[which], preferred_element_type=jnp.float32)]
    all_gather x1 -> x0, blocking collectives: 11.8 us -> none  [carried_in(): pieces = jax.tree.map(lambda part: lax.all_gather(part, axis), value)]
    select_n x7 -> x0, other arithmetic: 7.39 us -> none  [hop(): jnp.where(position < mine, new, old)]
    reduce_sum x2 -> x0, other arithmetic: 3.82 us -> none  [rms_scale(): mean_square = jnp.mean(widened * widened, axis=-1, keepdims=True)]
    convert_element_type x3 -> x0, other arithmetic: 3.08 us -> none  [the longest x1 1.96 us: local(): (residual.astype(jnp.float32) + ffn_summed).astype(jnp.bfloat16)]
  transfers between devices with their start and end apart: 5 -> 0, of which waited for: 5 -> 0; matrix products, arithmetic and copies ran while one was open for 5% -> 0% of each run, Pallas kernels for 0% -> 0%
where the time goes in v1:
time: 74.1 us; the launch traced here: 73.9 us
  Pallas kernels  69.2 us (93%)
  local copies, waits for them, and re-layouts  4.71 us (6%)
    pallas_call x1, Pallas kernels, local(): pl.pallas_call(functools.partial(kernel, blocks, steps), out_shape=jax.Sh...  69.2 us
    unnamed x2, local copies, waits for them, and re-layouts  4.71 us

profile of v1, /device:TPU:17, one launch (start us, length us, event | category | flops | bytes accessed | tf_op | source)
XLA Modules:
  0.0 73.9 jit_solution(3201719255070556519)
XLA Ops:
  0.0 1.6 %copy.9.fg = f32[512,8]{1,0:T(8,128)} copy(f32[512,8]{0,1:T(8,128)} %param.9) | data formatting | bytes 32768 | tf_op args[1]
  1.6 69.2 %shard_map.82 = bf16[512,2048]{1,0:T(8,128)(2,1)} custom-call(bf16[512,2048]{1,0:T(8,128)(2,1)} %tok_hbm.1, f32[512,8]{1,0:T(8,128)} %copy.9.fg, f32[8,512]{1,0:T(8,128)} %bitcast.3, f32[1,2048]{1,0:T(1,128)} %bitcast.4, bf16[3,2048,512]{2,1,0:T(8,128)(2,1)} %proj_hbm.1, bf16[512,2048]{1,0:T(8,128)(2,1)} %ow_hbm.1, f32[1,2048]{1,0:T(1,128)} %bitcast.5, ...), custom_call_target="tpu_custom_call" | custom-call | tf_op jit(solution)/shard_map/pallas_call | solution.py:369
  70.7 3.2 %copy.11 = bf16[512,2048]{1,0:T(8,128)(2,1)} copy(bf16[512,2048]{1,0:T(8,128)(2,1)} %shard_map.82) | data formatting | bytes 4194304

commit v2 on v1

--- a/solution.py
+++ b/solution.py
@@ -32,7 +32,7 @@
 
 def kernel(
     blocks, steps,
-    tok_hbm, fg, fgt, again, proj_hbm, ow_hbm, fgain, ew_hbm, dw_hbm,
+    tok_hbm, fgt, again, proj_hbm, ow_hbm, fgain, ew_hbm, dw_hbm,
     out_hbm,
     tok, wq, wk, wv, wo, wg, wu, wd,
     normed, q, k, v, att, ho, bd, es, el, ts, tl, tsb, tsl, trb, trl,
@@ -42,7 +42,7 @@
     wsem, sts, strv, d1s, d1r, x1s, x1r, ns, nr, d2s, d2r, x2s, x2r, osd, orv, olc,
 ):
     rows, width = tok.shape
-    heads = fg.shape[1]
+    heads = fgt.shape[0]
     pairs = heads // 2
     chunk = rows // CHUNKS
     half = chunk // 2
@@ -58,8 +58,9 @@
         (ow_hbm, wo), (ew_hbm.at[0], wg), (ew_hbm.at[1], wu), (dw_hbm, wd),
     )):
         copy = pltpu.make_async_copy(src, dst, wsem.at[at])
-        copy.start()
         loads.append(copy)
+    for at in range(3):
+        loads[at].start()
 
     barrier = pltpu.get_barrier_semaphore()
     for other in (partner, across):
@@ -74,7 +75,7 @@
         >= lax.broadcasted_iota(jnp.int32, (rows, rows), 1)
     ).astype(F32)
     ld[...] = lax.dot_general(
-        tri, fg[...], (((1,), (0,)), ((), ())),
+        tri, fgt[...], (((1,), (1,)), ((), ())),
         precision=lax.Precision.HIGHEST, preferred_element_type=F32,
     )
     ldt[...] = lax.dot_general(
@@ -83,6 +84,8 @@
     )
 
     loads[0].wait()
+    loads[3].start()
+    loads[4].start()
 
     def norm_chunk(r, carry):
         at = pl.ds(pl.multiple_of(r * chunk, chunk), chunk)
@@ -168,6 +171,8 @@
 
     if steps:
         send_state(0)
+    for at in (5, 6, 7):
+        loads[at].start()
     loads[3].wait()
     project(wq, q)
 
@@ -190,7 +195,7 @@
                 weights = (scores * 0.125 * jnp.exp(gaps)).astype(BF16)
                 sums.append(dot(weights, v[:reach, lanes]))
             att[at, lanes] = jnp.where(low, sums[0], sums[1])
-        if taken < steps:
+        if p % 2 and taken < steps:
             take_state(taken)
             taken += 1
     while taken < steps:
@@ -369,14 +374,14 @@
     return pl.pallas_call(
         functools.partial(kernel, blocks, steps),
         out_shape=jax.ShapeDtypeStruct((rows, width), BF16),
-        in_specs=[hbm, vmem, vmem, vmem, hbm, hbm, vmem, hbm, hbm],
+        in_specs=[hbm, vmem, vmem, hbm, hbm, vmem, hbm, hbm],
         out_specs=hbm,
         scratch_shapes=scratch,
         compiler_params=pltpu.CompilerParams(
             collective_id=0, has_side_effects=True, vmem_limit_bytes=64_000_000
         ),
     )(
-        tokens, forget, forget.T, attn_gain[None, :], projections, out_weight,
+        tokens, forget.T, attn_gain[None, :], projections, out_weight,
         ffn_gain[None, :], expand_weight, down_weight,
     )
 

time: 74.1 us -> 72.1 us (0.973); the launches traced: 73.9 us -> 71.1 us
  local copies, waits for them, and re-layouts: 4.71 us -> 3.16 us
  Pallas kernels: 69.2 us -> 67.9 us
    unnamed x2 -> x1, local copies, waits for them, and re-layouts: 4.71 us -> 3.16 us
    pallas_call x1, Pallas kernels: 69.2 us -> 67.9 us  [local(): pl.pallas_call(functools.partial(kernel, blocks, steps), out_shape=jax.Sh...]
where the time goes in v2:
time: 72.1 us; the launch traced here: 71.1 us
  Pallas kernels  67.9 us (94%)
  local copies, waits for them, and re-layouts  3.16 us (4%)
    pallas_call x1, Pallas kernels, local(): pl.pallas_call(functools.partial(kernel, blocks, steps), out_shape=jax.Sh...  67.9 us
    unnamed x1, local copies, waits for them, and re-layouts  3.16 us

profile of v2, /device:TPU:17, one launch (start us, length us, event | category | flops | bytes accessed | tf_op | source)
XLA Modules:
  0.0 71.1 jit_solution(7447334791919478524)
XLA Ops:
  0.0 67.9 %shard_map.82 = bf16[512,2048]{1,0:T(8,128)(2,1)} custom-call(bf16[512,2048]{1,0:T(8,128)(2,1)} %tok_hbm.1, f32[8,512]{1,0:T(8,128)} %bitcast.3, f32[1,2048]{1,0:T(1,128)} %bitcast.4, bf16[3,2048,512]{2,1,0:T(8,128)(2,1)} %proj_hbm.1, bf16[512,2048]{1,0:T(8,128)(2,1)} %ow_hbm.1, f32[1,2048]{1,0:T(1,128)} %bitcast.5, bf16[2,2048,1024]{2,1,0:T(8,128)(2,1)} %ew_hbm.1, ...), custom_call_target="tpu_custom_call" | custom-call | tf_op jit(solution)/shard_map/pallas_call | solution.py:374
  68.0 3.2 %copy.10 = bf16[512,2048]{1,0:T(8,128)(2,1)} copy(bf16[512,2048]{1,0:T(8,128)(2,1)} %shard_map.82) | data formatting | bytes 4194304

commit v3 on v2

--- a/solution.py
+++ b/solution.py
@@ -32,14 +32,14 @@
 
 def kernel(
     blocks, steps,
-    tok_hbm, fgt, again, proj_hbm, ow_hbm, fgain, ew_hbm, dw_hbm,
-    out_hbm,
-    tok, wq, wk, wv, wo, wg, wu, wd,
+    tok, fgt, again, proj_hbm, ow_hbm, fgain, ew_hbm, dw_hbm,
+    out,
+    wq, wk, wv, wo, wg, wu, wd,
     normed, q, k, v, att, ho, bd, es, el, ts, tl, tsb, tsl, trb, trl,
     part, own, dsend1, drecv1, xsend1, xrecv1, nf, res, hid,
-    dsend2, drecv2, xsend2, xrecv2, outb,
+    dsend2, drecv2, xsend2, xrecv2,
     ld, ldt,
-    wsem, sts, strv, d1s, d1r, x1s, x1r, ns, nr, d2s, d2r, x2s, x2r, osd, orv, olc,
+    wsem, sts, strv, d1s, d1r, x1s, x1r, ns, nr, d2s, d2r, x2s, x2r, osd, orv,
 ):
     rows, width = tok.shape
     heads = fgt.shape[0]
@@ -54,12 +54,12 @@
 
     loads = []
     for at, (src, dst) in enumerate((
-        (tok_hbm, tok), (proj_hbm.at[1], wk), (proj_hbm.at[2], wv), (proj_hbm.at[0], wq),
+        (proj_hbm.at[1], wk), (proj_hbm.at[2], wv), (proj_hbm.at[0], wq),
         (ow_hbm, wo), (ew_hbm.at[0], wg), (ew_hbm.at[1], wu), (dw_hbm, wd),
     )):
         copy = pltpu.make_async_copy(src, dst, wsem.at[at])
         loads.append(copy)
-    for at in range(3):
+    for at in range(2):
         loads[at].start()
 
     barrier = pltpu.get_barrier_semaphore()
@@ -83,10 +83,6 @@
         precision=lax.Precision.HIGHEST, preferred_element_type=F32,
     )
 
-    loads[0].wait()
-    loads[3].start()
-    loads[4].start()
-
     def norm_chunk(r, carry):
         at = pl.ds(pl.multiple_of(r * chunk, chunk), chunk)
         normed[at, :] = normalize(tok[at, :].astype(F32), again[...])
@@ -104,9 +100,11 @@
 
         lax.fori_loop(0, dst.shape[1] // tile, body, 0)
 
+    loads[0].wait()
+    for at in (2, 3):
+        loads[at].start()
+    project(wk, k)
     loads[1].wait()
-    project(wk, k)
-    loads[2].wait()
     project(wv, v)
 
     low = lax.broadcasted_iota(jnp.int32, (1, 128), 1) < 64
@@ -171,9 +169,9 @@
 
     if steps:
         send_state(0)
-    for at in (5, 6, 7):
+    for at in (4, 5, 6):
         loads[at].start()
-    loads[3].wait()
+    loads[2].wait()
     project(wq, q)
 
     span = rows // 2
@@ -195,9 +193,9 @@
                 weights = (scores * 0.125 * jnp.exp(gaps)).astype(BF16)
                 sums.append(dot(weights, v[:reach, lanes]))
             att[at, lanes] = jnp.where(low, sums[0], sums[1])
-        if p % 2 and taken < steps:
-            take_state(taken)
-            taken += 1
+            if 2 * p + piece in (1, pairs) and taken < steps:
+                take_state(taken)
+                taken += 1
     while taken < steps:
         take_state(taken)
         taken += 1
@@ -239,12 +237,9 @@
         return to(xsend2.at[r], xrecv2.at[r], x2s.at[r], x2r.at[r], across)
 
     def oc(r):
-        return to(outb.at[r], out_hbm.at[own_rows(r)], osd.at[r], orv.at[r], partner)
-
-    def ol(r):
-        return pltpu.make_async_copy(outb.at[r], out_hbm.at[own_rows(r)], olc.at[r])
-
-    loads[4].wait()
+        return to(out.at[own_rows(r)], out.at[own_rows(r)], osd.at[r], orv.at[r], partner)
+
+    loads[3].wait()
     wide = min(512, width)
 
     def attend(r, carry):
@@ -279,7 +274,7 @@
 
     lax.fori_loop(0, CHUNKS, attend_cross, 0)
     cross1(CHUNKS - 1)
-    for at in (5, 6, 7):
+    for at in (4, 5, 6):
         loads[at].wait()
 
     hidden_width = wg.shape[1]
@@ -315,9 +310,8 @@
     def finish(r, carry):
         x2(r).wait_recv()
         added = xsend2[r].astype(F32) + xrecv2[r].astype(F32)
-        outb[r] = (res[r].astype(F32) + added).astype(BF16)
+        out[own_rows(r), :] = (res[r].astype(F32) + added).astype(BF16)
         oc(r).start()
-        ol(r).start()
         return carry
 
     lax.fori_loop(0, CHUNKS, finish, 0)
@@ -326,7 +320,6 @@
         for copy in (d1(r), x1(r), nfc(r), d2(r), x2(r)):
             copy.wait_send()
         oc(r).wait()
-        ol(r).wait()
         return carry
 
     lax.fori_loop(0, CHUNKS, drain, 0)
@@ -351,7 +344,6 @@
     slots = max(steps, 1)
     piece = V((CHUNKS, half, width), BF16)
     scratch = [
-        V((rows, width), BF16),
         V((width, inner), BF16), V((width, inner), BF16), V((width, inner), BF16),
         V((inner, width), BF16),
         V((width, hidden), BF16), V((width, hidden), BF16), V((hidden, width), BF16),
@@ -365,20 +357,20 @@
         V((chunk, width), F32), V((CHUNKS, half, width), F32),
         piece, piece, piece, piece,
         V((rows, width), BF16), piece, V((chunk, hidden), BF16),
-        piece, piece, piece, piece, piece,
+        piece, piece, piece, piece,
         V((rows, heads), F32), V((heads, rows), F32),
         S((8,)), S((slots, 2)), S((slots, 2)),
-    ] + [S((CHUNKS,)) for _ in range(13)]
+    ] + [S((CHUNKS,)) for _ in range(12)]
     hbm = pl.BlockSpec(memory_space=pl.ANY)
     vmem = pl.BlockSpec(memory_space=pltpu.VMEM)
     return pl.pallas_call(
         functools.partial(kernel, blocks, steps),
         out_shape=jax.ShapeDtypeStruct((rows, width), BF16),
-        in_specs=[hbm, vmem, vmem, hbm, hbm, vmem, hbm, hbm],
-        out_specs=hbm,
+        in_specs=[vmem, vmem, vmem, hbm, hbm, vmem, hbm, hbm],
+        out_specs=vmem,
         scratch_shapes=scratch,
         compiler_params=pltpu.CompilerParams(
-            collective_id=0, has_side_effects=True, vmem_limit_bytes=64_000_000
+            collective_id=0, has_side_effects=True, vmem_limit_bytes=52_000_000
         ),
     )(
         tokens, forget.T, attn_gain[None, :], projections, out_weight,

time: 72.1 us -> 73.1 us (1.014)
  local copies, waits for them, and re-layouts: 3.16 us -> 5.02 us
    unnamed x1 -> x9, local copies, waits for them, and re-layouts: 3.16 us -> 5.02 us
where the time goes in v3:
time: 73.1 us; the launch traced here: 72.7 us
  Pallas kernels  67.7 us (93%)
  local copies, waits for them, and re-layouts  5.02 us (7%)
    pallas_call x1, Pallas kernels, local(): pl.pallas_call(functools.partial(kernel, blocks, steps), out_shape=jax.Sh...  67.7 us
    unnamed x9, local copies, waits for them, and re-layouts  5.02 us

profile of v3, /device:TPU:17, one launch (start us, length us, event | category | flops | bytes accessed | tf_op | source)
XLA Modules:
  0.0 72.7 jit_solution(5198876735184132863)
XLA Ops:
  0.0 0.0 copy-start
  0.0 1.6 %copy-done = bf16[512,2048]{1,0:T(8,128)(2,1)S(1)} copy-done((bf16[512,2048]{1,0:T(8,128)(2,1)S(1)}, bf16[512,2048]{1,0:T(8,128)(2,1)}, u32[]{:S(2)}) %copy-start) | copy-done | bytes 2097176
  1.6 0.0 copy-start.1
  1.6 0.7 copy-done.1
  2.3 0.0 copy-start.2
  2.3 0.7 copy-done.2
  3.0 0.0 copy-start.3
  3.0 0.7 copy-done.3
  3.7 67.7 %shard_map.82 = bf16[512,2048]{1,0:T(8,128)(2,1)S(1)} custom-call(bf16[512,2048]{1,0:T(8,128)(2,1)S(1)} %copy-done, f32[8,512]{1,0:T(8,128)S(1)} %bitcast.3, f32[1,2048]{1,0:T(1,128)S(1)} %bitcast.4, bf16[3,2048,512]{2,1,0:T(8,128)(2,1)} %proj_hbm.1, bf16[512,2048]{1,0:T(8,128)(2,1)} %ow_hbm.1, f32[1,2048]{1,0:T(1,128)S(1)} %bitcast.5, ...), custom_call_target="tpu_custom_call" | custom-call | tf_op jit(solution)/shard_map/pallas_call | solution.py:366
  71.4 1.3 %copy.10 = bf16[512,2048]{1,0:T(8,128)(2,1)} copy(bf16[512,2048]{1,0:T(8,128)(2,1)S(1)} %shard_map.82) | data formatting | bytes 4194304
Async XLA Ops:
  0.0 1.6 %copy-start = (bf16[512,2048]{1,0:T(8,128)(2,1)S(1)}, bf16[512,2048]{1,0:T(8,128)(2,1)}, u32[]{:S(2)}) copy-start(bf16[512,2048]{1,0:T(8,128)(2,1)} %tok.1) | copy-start | bytes 6291460
  1.6 0.7 copy-start.1
  2.3 0.7 copy-start.2
  3.0 0.7 copy-start.3
